TPU v7x, 256 devices: a whole 4x4x8 slice. The times are simulated.
256 devices in a mesh: seq: 8 (over y, x_lo), exp: 32 (over z, x_hi, core).
Axes of the slice: x: 4 (x_hi: 2, x_lo: 2; x = x_hi * 2 + x_lo), y: 4, z: 8, core: 2. Of those that a mesh axis runs over, the one named last changes fastest.
Arguments:
- tokens: bfloat16 [65536, 2048], P(('seq', 'exp')), may hold values from -128 to 128
- slot_embed: bfloat16 [2048, 256], P(None, 'exp'), may hold values from -0.397747564 to 0.397747564
- expert_in: bfloat16 [64, 2048, 4096], P('exp', None, 'seq'), may hold values from -0.125 to 0.125
- expert_out: bfloat16 [64, 4096, 2048], P('exp', 'seq'), may hold values from -0.09375 to 0.09375
- out_grad: bfloat16 [65536, 2048], P(('seq', 'exp')), may hold values from -0.59765625 to 0.59765625
Outputs:
- tok_grad: bfloat16 [65536, 2048], P(('seq', 'exp'))
- slot_grad: float32 [2048, 256], P('seq', 'exp')
All inputs are finite; a program needn't handle non-finite values.
Results may differ from a plain program's by a relative error of at most 0.024.
Values may be sent and summed in bfloat16 or wider, within the bound.
A program may use at most 64 MiB of HBM per device.

v0:
```python
from functools import partial
import functools
import jax
import jax.numpy as jnp
from jax import lax
from jax.sharding import Mesh
from jax.sharding import PartitionSpec as P

EXP = ("exp_0", "exp_1", "exp_2")
SEQ = ("seq_0", "seq_1")
SEQ_EXP = ("seq_0", "seq_1", "exp_0", "exp_1", "exp_2")


def split_up(x, dim, size):
    shape = x.shape
    blocks = x.reshape(*shape[:dim], size, shape[dim] // size, *shape[dim + 1 :])
    return jnp.moveaxis(blocks, dim, 0)


def sum_at_owner(x, axis, dim):
    size = lax.axis_size(axis)
    blocks = lax.all_to_all(split_up(x, dim, size), axis, 0, 0, tiled=True)
    return jnp.sum(blocks, axis=0)


def from_everyone(x, axis):
    copies = jnp.broadcast_to(x, (lax.axis_size(axis), *x.shape))
    return lax.all_to_all(copies, axis, split_axis=0, concat_axis=0, tiled=True)


def taken_together(x, axis):
    return from_everyone(x, axis).sum(axis=0)


def collected_together(x, axis):
    leaves = jax.tree.leaves(x)
    turns = sorted(range(len(leaves)), key=lambda k: -leaves[k].size)
    width = (1, *leaves[turns[0]].shape)[-1]
    lines = [
        jnp.pad(leaves[k].reshape(-1), (0, -leaves[k].size % width)).reshape(-1, width)
        for k in turns
    ]
    both, at, found = (lax.all_gather(jnp.concatenate(lines), axis), 0, {})
    for k, line in zip(turns, lines):
        section = both[:, at : at + len(line)].reshape(len(both), -1)
        found[k] = section[:, : leaves[k].size].reshape(-1, *leaves[k].shape)
        at += len(line)
    numbers = iter(range(len(leaves)))
    return jax.tree.map(lambda _: found[next(numbers)], x)


def joined_all(x, axes, combine):
    for axis in axes:
        pieces = collected_together(x, axis)
        x = jax.tree.map(lambda part: part[0], pieces)
        for k in range(1, lax.axis_size(axis)):
            x = combine(x, jax.tree.map(lambda part: part[k], pieces))
    return x


def one_axis_at_a_time(x, axes):
    return functools.reduce(lax.psum, axes, x)


def contract_rows(left, right):
    return lax.dot_general(
        left, right, (((0,), (0,)), ((), ())), preferred_element_type=jnp.float32
    )


def contract_cols(left, right):
    return lax.dot_general(
        left, right, (((1,), (1,)), ((), ())), preferred_element_type=jnp.float32
    )


def merge_stats(first_pair, second_pair):
    top_value = jnp.maximum(first_pair[0], second_pair[0])
    summed = first_pair[1] * jnp.exp(first_pair[0] - top_value) + second_pair[1] * jnp.exp(
        second_pair[0] - top_value
    )
    return (top_value, summed)


def owner_sum(partial_rows):
    owned = sum_at_owner(partial_rows, EXP, 0)
    return taken_together(owned, SEQ)


def shards(tokens, slot_embed, expert_in, expert_out, out_grad):
    experts_here = expert_in.shape[0]
    model_width = tokens.shape[1]
    slot_table = lax.all_gather(slot_embed, EXP, axis=1, tiled=True)
    logits = jnp.dot(tokens, slot_table, preferred_element_type=jnp.float32)
    local_top = jnp.max(logits, axis=0)
    local_total = jnp.sum(jnp.exp(logits - local_top), axis=0)
    col_top, col_total = joined_all((local_top, local_total), SEQ_EXP, merge_stats)
    dispatch = jnp.exp(logits - col_top) / col_total
    dispatch_b = dispatch.astype(jnp.bfloat16)
    combine_w = jax.nn.softmax(logits, axis=1)
    combine_b = combine_w.astype(jnp.bfloat16)
    slot_sum = owner_sum(contract_rows(dispatch_b, tokens))
    slot_in = slot_sum.astype(jnp.bfloat16).reshape(experts_here, -1, model_width)
    pre_act = jnp.einsum("esd,edh->esh", slot_in, expert_in, preferred_element_type=jnp.float32)
    hidden = jax.nn.gelu(pre_act, approximate=True).astype(jnp.bfloat16)
    out_part = jnp.einsum("esh,ehd->esd", hidden, expert_out, preferred_element_type=jnp.float32)
    slot_out = taken_together(out_part, SEQ).astype(jnp.bfloat16).reshape(-1, model_width)
    slot_all = lax.all_gather(slot_out, EXP, axis=0, tiled=True)
    comb_grad = contract_cols(out_grad, slot_all)
    grad_out = owner_sum(contract_rows(combine_b, out_grad))
    grad_out = grad_out.astype(jnp.bfloat16).reshape(experts_here, -1, model_width)
    hid_grad = jnp.einsum("esd,ehd->esh", grad_out, expert_out, preferred_element_type=jnp.float32)
    _, pullback = jax.vjp(partial(jax.nn.gelu, approximate=True), pre_act)
    act_grad = pullback(hid_grad)[0].astype(jnp.bfloat16)
    in_part = jnp.einsum("esh,edh->esd", act_grad, expert_in, preferred_element_type=jnp.float32)
    grad_own = taken_together(in_part, SEQ).astype(jnp.bfloat16).reshape(-1, model_width)
    grad_all = lax.all_gather(grad_own, EXP, axis=0, tiled=True)
    disp_grad = contract_cols(tokens, grad_all)
    centre_local = jnp.sum(dispatch_b.astype(jnp.float32) * disp_grad, axis=0)
    centre = one_axis_at_a_time(centre_local, SEQ_EXP)
    comb_mean = jnp.sum(combine_w * comb_grad, axis=1, keepdims=True)
    logit_grad = dispatch * (disp_grad - centre) + combine_w * (comb_grad - comb_mean)
    logit_b = logit_grad.astype(jnp.bfloat16)
    tok_grad = jnp.dot(dispatch_b, grad_all, preferred_element_type=jnp.float32) + contract_cols(
        logit_b, slot_table
    )
    table_part = contract_rows(tokens, logit_b)
    table_owned = sum_at_owner(table_part, EXP, 1)
    slot_grad = sum_at_owner(table_owned, SEQ, 0)
    return (tok_grad.astype(jnp.bfloat16), slot_grad)


def solution(mesh):
    torus = Mesh(mesh.devices.reshape(4, 2, 8, 2, 2), ("seq_0", "seq_1", "exp_0", "exp_1", "exp_2"))
    placed = (
        P(SEQ_EXP, None),
        P(None, EXP),
        P(EXP, None, SEQ),
        P(EXP, SEQ, None),
        P(SEQ_EXP, None),
    )
    return jax.shard_map(
        shards,
        mesh=torus,
        in_specs=placed,
        out_specs=(P(SEQ_EXP, None), P(SEQ, EXP)),
        check_vma=False,
    )
```

profile of v0, /device:TPU:4, one launch (start us, length us, event | category | flops | bytes accessed | tf_op | source)
XLA Modules:
  0.0 532.9 jit_solution(1406648568173986912)
XLA Ops:
  7.2 0.0 copy-start
  7.2 0.0 all-gather.14.cloned.1.call-start
  7.2 0.7 all-gather.14.cloned.1.call-update
  7.9 81.8 %all-gather.14.cloned.1.call-done = bf16[2048,256]{0,1:T(8,128)(2,1)} async-done(((bf16[2048,8]{0,1:T(8,128)(2,1)}), bf16[2048,256]{0,1:T(8,128)(2,1)}) %all-gather.14.cloned.1.call-update) | async-done | bytes 1048592 | tf_op jit(solution)/shard_map/all_gather | solution.py:93
  89.7 0.0 copy-done
  89.7 1.8 fusion.85
  91.5 0.2 fusion.2
  91.7 11.2 %all-gather.5 = f32[4,2,256]{2,1,0:T(2,128)S(1)} all-gather(f32[1,2,256]{2,1,0:T(2,128)S(1)} %maximum_bitcast_fusion), channel_id=2, replica_groups=mesh['seq_0'=4,'seq_1'=2,'exp_0'=8,'exp_1'=2,'exp_2'=2] {'seq_0'}, dimensions={0}, use_global_device_ids=true | all-gather | bytes 10240 | tf_op jit(solution)/shard_map/all_gather | solution.py:43
  102.9 4.4 all-gather.6
  107.3 21.6 %all-gather.7 = f32[8,2,256]{2,1,0:T(2,128)S(1)} all-gather(f32[1,2,256]{2,1,0:T(2,128)S(1)} %maximum_bitcast_fusion.2), channel_id=4, replica_groups=mesh['seq_0'=4,'seq_1'=2,'exp_0'=8,'exp_1'=2,'exp_2'=2] {'exp_0'}, dimensions={0}, use_global_device_ids=true | all-gather | bytes 18432 | tf_op jit(solution)/shard_map/all_gather | solution.py:43
  128.9 5.9 %all-gather.8 = f32[2,2,256]{2,1,0:T(2,128)S(1)} all-gather(f32[1,2,256]{2,1,0:T(2,128)S(1)} %maximum_bitcast_fusion.3), channel_id=5, replica_groups=mesh['seq_0'=4,'seq_1'=2,'exp_0'=8,'exp_1'=2,'exp_2'=2] {'exp_1'}, dimensions={0}, use_global_device_ids=true | all-gather | bytes 6144 | tf_op jit(solution)/shard_map/all_gather | solution.py:43
  134.8 1.8 all-gather.9
  136.7 1.8 convolution_bitcast_fusion.1
  138.4 7.1 %all-to-all-start.2 = ((f32[32,8,2048]{2,1,0:T(8,128)}), f32[32,8,2048]{2,1,0:T(8,128)S(1)}, u32[]{:S(2)}, u32[]{:S(2)}) async-start(f32[32,8,2048]{2,1,0:T(8,128)} %convolution_bitcast_fusion.1), calls=%async_computation.2 | async-start | bytes 4194304 | tf_op jit(solution)/shard_map/all_to_all | solution.py:22
  145.6 3.2 convolution_bitcast_fusion.2
  148.7 47.0 %all-to-all-done.2 = f32[32,8,2048]{2,1,0:T(8,128)S(1)} async-done(((f32[32,8,2048]{2,1,0:T(8,128)}), f32[32,8,2048]{2,1,0:T(8,128)S(1)}, u32[]{:S(2)}, u32[]{:S(2)}) %all-to-all-start.2) | async-done | bytes 2097184 | tf_op jit(solution)/shard_map/all_to_all | solution.py:22
  195.7 1.3 copy-done.1
  197.0 6.3 %all-to-all-start = ((f32[32,8,2048]{2,1,0:T(8,128)}), f32[32,8,2048]{2,1,0:T(8,128)S(1)}, u32[]{:S(2)}, u32[]{:S(2)}) async-start(f32[32,8,2048]{2,1,0:T(8,128)} %convolution_bitcast_fusion.2), calls=%async_computation | async-start | bytes 4194304 | tf_op jit(solution)/shard_map/all_to_all | solution.py:22
  203.3 1.7 reduce_sum.112
  205.0 48.5 %all-to-all-done = f32[32,8,2048]{2,1,0:T(8,128)S(1)} async-done(((f32[32,8,2048]{2,1,0:T(8,128)}), f32[32,8,2048]{2,1,0:T(8,128)S(1)}, u32[]{:S(2)}, u32[]{:S(2)}) %all-to-all-start) | async-done | bytes 2097184 | tf_op jit(solution)/shard_map/all_to_all | solution.py:22
  253.5 0.8 broadcast_in_dim.9
  254.3 4.2 all-to-all-start.3
  258.5 0.1 reduce_sum.110
  258.6 10.5 %all-to-all-done.3 = f32[8,8,2048]{2,1,0:T(8,128)} async-done(((f32[8,8,2048]{2,1,0:T(8,128)}), f32[8,8,2048]{2,1,0:T(8,128)}, u32[]{:S(2)}, u32[]{:S(2)}) %all-to-all-start.3) | async-done | bytes 524320 | tf_op jit(solution)/shard_map/all_to_all | solution.py:28
  269.1 0.8 broadcast_in_dim.8
  269.9 3.5 all-to-all-start.1
  273.4 0.0 all-gather.16.cloned.1.call-start
  273.4 1.1 reduce_sum.113
  274.5 8.1 %all-to-all-done.1 = f32[8,8,2048]{2,1,0:T(8,128)S(1)} async-done(((f32[8,8,2048]{2,1,0:T(8,128)}), f32[8,8,2048]{2,1,0:T(8,128)S(1)}, u32[]{:S(2)}, u32[]{:S(2)}) %all-to-all-start.1) | async-done | bytes 524320 | tf_op jit(solution)/shard_map/all_to_all | solution.py:28
  282.7 2.8 fusion.96
  285.6 5.7 %fusion.12 = f32[2,4,2048]{2,1,0:T(4,128)S(1)} fusion(bf16[2,2048,512]{2,1,0:T(8,128)(2,1)} %param.7, f32[2,4,512]{2,1,0:T(4,128)S(1)} %fusion.96, bf16[2,4,2048]{2,1,0:T(4,128)(2,1)S(1)} %convert_element_type.52, bf16[2,512,2048]{2,1,0:T(8,128)(2,1)} %param.8), kind=kOutput, calls=%fused_computation.27 | convolution fusion | flops 33636352 | bytes 8503296 | tf_op jit(solution)/shard_map/esh,edh->esd/dot_general | solution.py:115
  291.3 0.1 broadcast_in_dim.10
  291.4 11.4 %all_to_all.40 = f32[8,2,4,2048]{3,2,1,0:T(4,128)S(1)} all-to-all(f32[8,2,4,2048]{3,2,1,0:T(4,128)S(1)} %broadcast_in_dim.10), channel_id=1, replica_groups=mesh['seq_0'=4,'seq_1'=2,'exp_0'=8,'exp_1'=2,'exp_2'=2] {'seq_0','seq_1'}, dimensions={0} | all-to-all | bytes 1048576 | tf_op jit(solution)/shard_map/all_to_all | solution.py:28
  302.8 0.1 reduce_sum.114
  302.9 0.6 convert_element_type.57
  303.5 0.0 all-gather.16.cloned.1.call-update
  303.6 0.0 copy-start.2
  303.6 0.0 all-gather.18.cloned.1.call-start
  303.6 2.9 fusion.14
  306.5 0.1 broadcast_in_dim.22
  306.7 11.6 %all_to_all.41 = f32[8,2,4,2048]{3,2,1,0:T(4,128)S(1)} all-to-all(f32[8,2,4,2048]{3,2,1,0:T(4,128)S(1)} %broadcast_in_dim.22), channel_id=1, replica_groups=mesh['seq_0'=4,'seq_1'=2,'exp_0'=8,'exp_1'=2,'exp_2'=2] {'seq_0','seq_1'}, dimensions={0} | all-to-all | bytes 1048576 | tf_op jit(solution)/shard_map/all_to_all | solution.py:28
  318.2 0.1 reduce_sum.116
  318.3 0.6 convert_element_type.61
  318.9 0.0 all-gather.18.cloned.1.call-update
  319.0 55.8 %all-gather.16.cloned.1.call-done = bf16[256,2048]{1,0:T(8,128)(2,1)} async-done(((bf16[8,2048]{1,0:T(8,128)(2,1)}), bf16[256,2048]{1,0:T(8,128)(2,1)}) %all-gather.16.cloned.1.call-update) | async-done | bytes 1048592 | tf_op jit(solution)/shard_map/all_gather | solution.py:117
  374.8 1.7 multiply_reduce_fusion.1
  376.5 0.0 copy-start.3
  376.5 10.5 %psum.35 = f32[256]{0:T(256)S(1)} all-reduce(f32[256]{0:T(256)S(1)} %get-tuple-element.23), channel_id=1, replica_groups=mesh['seq_0'=4,'seq_1'=2,'exp_0'=8,'exp_1'=2,'exp_2'=2] {'seq_0'}, use_global_device_ids=true, to_apply=%region_10.11 | all-reduce | flops 256 | bytes 2048 | tf_op jit(solution)/shard_map/psum | solution.py:62
  387.0 4.9 psum.36
  391.9 15.5 %psum.37 = f32[256]{0:T(256)S(1)} all-reduce(f32[256]{0:T(256)S(1)} %psum.36), channel_id=1, replica_groups=mesh['seq_0'=4,'seq_1'=2,'exp_0'=8,'exp_1'=2,'exp_2'=2] {'exp_0'}, use_global_device_ids=true, to_apply=%region_12.13 | all-reduce | flops 256 | bytes 2048 | tf_op jit(solution)/shard_map/psum | solution.py:62
  407.5 6.4 %psum.38 = f32[256]{0:T(256)S(1)} all-reduce(f32[256]{0:T(256)S(1)} %psum.37), channel_id=1, replica_groups=mesh['seq_0'=4,'seq_1'=2,'exp_0'=8,'exp_1'=2,'exp_2'=2] {'exp_1'}, use_global_device_ids=true, to_apply=%region_13.14 | all-reduce | flops 256 | bytes 2048 | tf_op jit(solution)/shard_map/psum | solution.py:62
  413.9 2.4 psum.39
  416.4 35.9 %all-gather.18.cloned.1.call-done = bf16[256,2048]{1,0:T(8,128)(2,1)} async-done(((bf16[8,2048]{1,0:T(8,128)(2,1)}), bf16[256,2048]{1,0:T(8,128)(2,1)}) %all-gather.18.cloned.1.call-update) | async-done | bytes 1048592 | tf_op jit(solution)/shard_map/all_gather | solution.py:108
  452.3 0.0 copy-done.2
  452.3 1.8 multiply_reduce_fusion
  454.1 1.9 convolution_bitcast_fusion
  456.0 7.6 %all-to-all-start.6 = ((f32[32,2048,8]{1,2,0:T(8,128)}), f32[32,2048,8]{1,2,0:T(8,128)S(1)}, u32[]{:S(2)}, u32[]{:S(2)}) async-start(f32[32,2048,8]{1,2,0:T(8,128)} %convolution_bitcast_fusion), calls=%async_computation.6 | async-start | bytes 4194304 | tf_op jit(solution)/shard_map/all_to_all | solution.py:22
  463.6 3.0 fusion.93
  466.6 47.1 %all-to-all-done.6 = f32[32,2048,8]{1,2,0:T(8,128)S(1)} async-done(((f32[32,2048,8]{1,2,0:T(8,128)}), f32[32,2048,8]{1,2,0:T(8,128)S(1)}, u32[]{:S(2)}, u32[]{:S(2)}) %all-to-all-start.6) | async-done | bytes 2097184 | tf_op jit(solution)/shard_map/all_to_all | solution.py:22
  513.8 0.7 reduce_sum.118
  514.5 4.9 all-to-all-start.7
  519.4 3.6 fusion
  523.0 2.8 all-to-all-done.7
  525.8 0.6 reduce_sum.119
  (18 shorter events, 0.2 us)
Async XLA Ops:
  7.2 82.5 %copy-start = (bf16[256,2048]{1,0:T(8,128)(2,1)S(1)}, bf16[256,2048]{1,0:T(8,128)(2,1)}, u32[]{:S(2)}) copy-start(bf16[256,2048]{1,0:T(8,128)(2,1)} %param.5) | copy-start | bytes 3145732
  7.2 82.5 %all-gather.14.cloned.1.call-start = ((), (), s32[]{:S(2)}) async-start(), calls=%async_computation.8 | async-start | bytes 1081344 | tf_op jit(solution)/shard_map/all_gather | solution.py:93
  138.4 57.3 %all-to-all-start.2 = ((f32[32,8,2048]{2,1,0:T(8,128)}), f32[32,8,2048]{2,1,0:T(8,128)S(1)}, u32[]{:S(2)}, u32[]{:S(2)}) async-start(f32[32,8,2048]{2,1,0:T(8,128)} %convolution_bitcast_fusion.1), calls=%async_computation.2 | async-start | bytes 4194304 | tf_op jit(solution)/shard_map/all_to_all | solution.py:22
  195.7 1.3 copy-start.1
  197.0 56.4 %all-to-all-start = ((f32[32,8,2048]{2,1,0:T(8,128)}), f32[32,8,2048]{2,1,0:T(8,128)S(1)}, u32[]{:S(2)}, u32[]{:S(2)}) async-start(f32[32,8,2048]{2,1,0:T(8,128)} %convolution_bitcast_fusion.2), calls=%async_computation | async-start | bytes 4194304 | tf_op jit(solution)/shard_map/all_to_all | solution.py:22
  254.3 14.8 %all-to-all-start.3 = ((f32[8,8,2048]{2,1,0:T(8,128)}), f32[8,8,2048]{2,1,0:T(8,128)}, u32[]{:S(2)}, u32[]{:S(2)}) async-start(f32[8,8,2048]{2,1,0:T(8,128)} %broadcast_in_dim.9), calls=%async_computation.3 | async-start | bytes 1048576 | tf_op jit(solution)/shard_map/all_to_all | solution.py:28
  269.9 12.8 %all-to-all-start.1 = ((f32[8,8,2048]{2,1,0:T(8,128)}), f32[8,8,2048]{2,1,0:T(8,128)S(1)}, u32[]{:S(2)}, u32[]{:S(2)}) async-start(f32[8,8,2048]{2,1,0:T(8,128)} %broadcast_in_dim.8), calls=%async_computation.1 | async-start | bytes 1048576 | tf_op jit(solution)/shard_map/all_to_all | solution.py:28
  273.4 101.4 %all-gather.16.cloned.1.call-start = ((), (), s32[]{:S(2)}) async-start(), calls=%async_computation.9 | async-start | bytes 1081344 | tf_op jit(solution)/shard_map/all_gather | solution.py:117
  303.6 148.7 %copy-start.2 = (bf16[256,2048]{1,0:T(8,128)(2,1)S(1)}, bf16[256,2048]{1,0:T(8,128)(2,1)}, u32[]{:S(2)}) copy-start(bf16[256,2048]{1,0:T(8,128)(2,1)} %param.9) | copy-start | bytes 3145732
  303.6 148.7 %all-gather.18.cloned.1.call-start = ((), (), s32[]{:S(2)}) async-start(), calls=%async_computation.10 | async-start | bytes 1081344 | tf_op jit(solution)/shard_map/all_gather | solution.py:108
  376.5 79.5 %copy-start.3 = (f32[256,256]{1,0:T(8,128)}, f32[256,256]{1,0:T(8,128)S(1)}, u32[]{:S(2)}) copy-start(f32[256,256]{1,0:T(8,128)S(1)} %get-tuple-element.24) | copy-start | bytes 786436
  454.1 1.9 copy-start.4
  456.0 57.7 %all-to-all-start.6 = ((f32[32,2048,8]{1,2,0:T(8,128)}), f32[32,2048,8]{1,2,0:T(8,128)S(1)}, u32[]{:S(2)}, u32[]{:S(2)}) async-start(f32[32,2048,8]{1,2,0:T(8,128)} %convolution_bitcast_fusion), calls=%async_computation.6 | async-start | bytes 4194304 | tf_op jit(solution)/shard_map/all_to_all | solution.py:22
  514.5 11.3 %all-to-all-start.7 = ((f32[8,256,8]{1,2,0:T(8,128)}), f32[8,256,8]{1,2,0:T(8,128)S(1)}, u32[]{:S(2)}, u32[]{:S(2)}) async-start(f32[8,256,8]{1,2,0:T(8,128)} %bitcast.50), calls=%async_computation.7 | async-start | bytes 131072 | tf_op jit(solution)/shard_map/all_to_all | solution.py:22
Sparse Core Ops, SparseCore 0:
  10.8 78.8 all-gather.13
  303.7 71.0 all-gather.15
  377.6 74.6 all-gather.17
where the time goes:
time: 534 us; the launch traced here: 533 us
  waiting for transfers between devices  338 us (63%)
  blocking collectives  108 us (20%)
  starting transfers between devices  33.7 us (6%)
  matrix products  30.2 us (6%)
  between operations  13.9 us (3%)
    all_to_all x4, waiting for transfers between devices, sum_at_owner(): blocks = lax.all_to_all(split_up(x, dim, size), axis, 0, 0, tiled=True)  145 us
    all_gather x1, waiting for transfers between devices, shards(): slot_table = lax.all_gather(slot_embed, EXP, axis=1, tiled=True)  81.8 us
    all_gather x1, waiting for transfers between devices, shards(): grad_all = lax.all_gather(grad_own, EXP, axis=0, tiled=True)  55.8 us
    all_gather x5, blocking collectives, collected_together(): both, at, found = (lax.all_gather(jnp.concatenate(lines), axis), 0, {})  44.8 us
    psum x5, blocking collectives, one_axis_at_a_time(): return functools.reduce(lax.psum, axes, x)  39.9 us
    all_gather x1, waiting for transfers between devices, shards(): slot_all = lax.all_gather(slot_out, EXP, axis=0, tiled=True)  35.9 us
    all_to_all x4, starting transfers between devices, sum_at_owner(): blocks = lax.all_to_all(split_up(x, dim, size), axis, 0, 0, tiled=True)  25.9 us
    all_to_all x2, blocking collectives, from_everyone(): return lax.all_to_all(copies, axis, split_axis=0, concat_axis=0, tiled=True)  23 us
  transfers between devices with their start and end apart: 9, of which 9 were waited for; matrix products, arithmetic and copies ran while one was open for 3% of the time, Pallas kernels for 0%

commit v1 on v0

--- a/solution.py
+++ b/solution.py
@@ -105,7 +105,10 @@
     hidden = jax.nn.gelu(pre_act, approximate=True).astype(jnp.bfloat16)
     out_part = jnp.einsum("esh,ehd->esd", hidden, expert_out, preferred_element_type=jnp.float32)
     slot_out = taken_together(out_part, SEQ).astype(jnp.bfloat16).reshape(-1, model_width)
-    slot_all = lax.all_gather(slot_out, EXP, axis=0, tiled=True)
+    peers = lax.axis_size(EXP)
+    shards_2 = jnp.stack([slot_out for _ in range(peers)])
+    shards_2 = lax.all_to_all(shards_2, EXP, split_axis=0, concat_axis=0)
+    slot_all = jnp.concatenate(shards_2, axis=0)
     comb_grad = contract_cols(out_grad, slot_all)
     grad_out = owner_sum(contract_rows(combine_b, out_grad))
     grad_out = grad_out.astype(jnp.bfloat16).reshape(experts_here, -1, model_width)

time: 534 us -> 512 us (0.959)
  blocking collectives: 108 us -> 84.6 us
  waiting for transfers between devices: 338 us -> 323 us
  starting transfers between devices: 33.7 us -> 46.2 us
    all_gather x1 -> x0, waiting for transfers between devices: 35.9 us -> none  [shards(): slot_all = lax.all_gather(slot_out, EXP, axis=0, tiled=True)]
    all_to_all x2 -> x0, blocking collectives: 23 us -> none  [from_everyone(): return lax.all_to_all(copies, axis, split_axis=0, concat_axis=0, tiled=True)]
    all_to_all x2 -> x4, waiting for transfers between devices: 18.6 us -> 32.4 us  [from_everyone(): return lax.all_to_all(copies, axis, split_axis=0, concat_axis=0, tiled=True)]
    all_to_all x2 -> x4, starting transfers between devices: 7.65 us -> 14.8 us  [from_everyone(): return lax.all_to_all(copies, axis, split_axis=0, concat_axis=0, tiled=True)]
    all_gather x1, waiting for transfers between devices: 55.8 us -> 62.5 us  [shards(): grad_all = lax.all_gather(grad_own, EXP, axis=0, tiled=True)]
    all_to_all x0 -> x1, starting transfers between devices: none -> 5.99 us  [shards(): shards_2 = lax.all_to_all(shards_2, EXP, split_axis=0, concat_axis=0)]
  transfers between devices with their start and end apart: 9 -> 11, of which waited for: 9 -> 10; matrix products, arithmetic and copies ran while one was open for 3% -> 4% of each run, Pallas kernels for 0% -> 0%
where the time goes in v1:
time: 512 us; the launch traced here: 510 us
  waiting for transfers between devices  323 us (63%)
  blocking collectives  84.6 us (17%)
  starting transfers between devices  46.2 us (9%)
  matrix products  30.6 us (6%)
  between operations  14.2 us (3%)
  local copies, waits for them, and re-layouts  7.24 us (1%)
    all_to_all x4, waiting for transfers between devices, sum_at_owner(): blocks = lax.all_to_all(split_up(x, dim, size), axis, 0, 0, tiled=True)  145 us
    all_gather x1, waiting for transfers between devices, shards(): slot_table = lax.all_gather(slot_embed, EXP, axis=1, tiled=True)  81.8 us
    all_gather x1, waiting for transfers between devices, shards(): grad_all = lax.all_gather(grad_own, EXP, axis=0, tiled=True)  62.5 us
    all_gather x5, blocking collectives, collected_together(): both, at, found = (lax.all_gather(jnp.concatenate(lines), axis), 0, {})  44.8 us
    psum x5, blocking collectives, one_axis_at_a_time(): return functools.reduce(lax.psum, axes, x)  39.8 us
    all_to_all x4, waiting for transfers between devices, from_everyone(): return lax.all_to_all(copies, axis, split_axis=0, concat_axis=0, tiled=True)  32.4 us
    all_to_all x4, starting transfers between devices, sum_at_owner(): blocks = lax.all_to_all(split_up(x, dim, size), axis, 0, 0, tiled=True)  25.4 us
    all_to_all x4, starting transfers between devices, from_everyone(): return lax.all_to_all(copies, axis, split_axis=0, concat_axis=0, tiled=True)  14.8 us
  transfers between devices with their start and end apart: 11, of which 10 were waited for; matrix products, arithmetic and copies ran while one was open for 4% of the time, Pallas kernels for 0%

profile of v1, /device:TPU:4, one launch (start us, length us, event | category | flops | bytes accessed | tf_op | source)
XLA Modules:
  0.0 510.2 jit_solution(1346751070956218530)
XLA Ops:
  7.2 0.0 copy-start
  7.2 0.0 all-gather.13.cloned.1.call-start
  7.2 0.7 all-gather.13.cloned.1.call-update
  7.9 81.8 %all-gather.13.cloned.1.call-done = bf16[2048,256]{0,1:T(8,128)(2,1)} async-done(((bf16[2048,8]{0,1:T(8,128)(2,1)}), bf16[2048,256]{0,1:T(8,128)(2,1)}) %all-gather.13.cloned.1.call-update) | async-done | bytes 1048592 | tf_op jit(solution)/shard_map/all_gather | solution.py:93
  89.7 0.0 copy-done
  89.7 1.8 fusion.86
  91.5 0.2 fusion.3
  91.7 11.2 %all-gather.5 = f32[4,2,256]{2,1,0:T(2,128)S(1)} all-gather(f32[1,2,256]{2,1,0:T(2,128)S(1)} %maximum_bitcast_fusion), channel_id=2, replica_groups=mesh['seq_0'=4,'seq_1'=2,'exp_0'=8,'exp_1'=2,'exp_2'=2] {'seq_0'}, dimensions={0}, use_global_device_ids=true | all-gather | bytes 10240 | tf_op jit(solution)/shard_map/all_gather | solution.py:43
  102.9 4.4 all-gather.6
  107.3 21.6 %all-gather.7 = f32[8,2,256]{2,1,0:T(2,128)S(1)} all-gather(f32[1,2,256]{2,1,0:T(2,128)S(1)} %maximum_bitcast_fusion.2), channel_id=4, replica_groups=mesh['seq_0'=4,'seq_1'=2,'exp_0'=8,'exp_1'=2,'exp_2'=2] {'exp_0'}, dimensions={0}, use_global_device_ids=true | all-gather | bytes 18432 | tf_op jit(solution)/shard_map/all_gather | solution.py:43
  128.9 5.9 %all-gather.8 = f32[2,2,256]{2,1,0:T(2,128)S(1)} all-gather(f32[1,2,256]{2,1,0:T(2,128)S(1)} %maximum_bitcast_fusion.3), channel_id=5, replica_groups=mesh['seq_0'=4,'seq_1'=2,'exp_0'=8,'exp_1'=2,'exp_2'=2] {'exp_1'}, dimensions={0}, use_global_device_ids=true | all-gather | bytes 6144 | tf_op jit(solution)/shard_map/all_gather | solution.py:43
  134.8 1.8 all-gather.9
  136.7 1.8 convolution_bitcast_fusion.1
  138.4 7.1 %all-to-all-start.2 = ((f32[32,8,2048]{2,1,0:T(8,128)}), f32[32,8,2048]{2,1,0:T(8,128)S(1)}, u32[]{:S(2)}, u32[]{:S(2)}) async-start(f32[32,8,2048]{2,1,0:T(8,128)} %convolution_bitcast_fusion.1), calls=%async_computation.2 | async-start | bytes 4194304 | tf_op jit(solution)/shard_map/all_to_all | solution.py:22
  145.6 3.2 convolution_bitcast_fusion.2
  148.7 47.0 %all-to-all-done.2 = f32[32,8,2048]{2,1,0:T(8,128)S(1)} async-done(((f32[32,8,2048]{2,1,0:T(8,128)}), f32[32,8,2048]{2,1,0:T(8,128)S(1)}, u32[]{:S(2)}, u32[]{:S(2)}) %all-to-all-start.2) | async-done | bytes 2097184 | tf_op jit(solution)/shard_map/all_to_all | solution.py:22
  195.7 1.3 copy-done.1
  197.0 6.3 %all-to-all-start = ((f32[32,8,2048]{2,1,0:T(8,128)}), f32[32,8,2048]{2,1,0:T(8,128)S(1)}, u32[]{:S(2)}, u32[]{:S(2)}) async-start(f32[32,8,2048]{2,1,0:T(8,128)} %convolution_bitcast_fusion.2), calls=%async_computation | async-start | bytes 4194304 | tf_op jit(solution)/shard_map/all_to_all | solution.py:22
  203.3 1.7 reduce_sum.112
  205.0 48.5 %all-to-all-done = f32[32,8,2048]{2,1,0:T(8,128)S(1)} async-done(((f32[32,8,2048]{2,1,0:T(8,128)}), f32[32,8,2048]{2,1,0:T(8,128)S(1)}, u32[]{:S(2)}, u32[]{:S(2)}) %all-to-all-start) | async-done | bytes 2097184 | tf_op jit(solution)/shard_map/all_to_all | solution.py:22
  253.5 0.8 broadcast_in_dim.9
  254.3 4.2 all-to-all-start.3
  258.5 0.1 reduce_sum.110
  258.6 10.5 %all-to-all-done.3 = f32[8,8,2048]{2,1,0:T(8,128)} async-done(((f32[8,8,2048]{2,1,0:T(8,128)}), f32[8,8,2048]{2,1,0:T(8,128)}, u32[]{:S(2)}, u32[]{:S(2)}) %all-to-all-start.3) | async-done | bytes 524320 | tf_op jit(solution)/shard_map/all_to_all | solution.py:28
  269.1 0.8 broadcast_in_dim.8
  269.9 3.5 all-to-all-start.1
  273.4 1.1 reduce_sum.113
  274.5 8.2 %all-to-all-done.1 = f32[8,8,2048]{2,1,0:T(8,128)S(1)} async-done(((f32[8,8,2048]{2,1,0:T(8,128)}), f32[8,8,2048]{2,1,0:T(8,128)S(1)}, u32[]{:S(2)}, u32[]{:S(2)}) %all-to-all-start.1) | async-done | bytes 524320 | tf_op jit(solution)/shard_map/all_to_all | solution.py:28
  282.7 2.8 fusion.97
  285.6 5.7 %fusion.13 = f32[2,4,2048]{2,1,0:T(4,128)S(1)} fusion(bf16[2,2048,512]{2,1,0:T(8,128)(2,1)} %param.7, f32[2,4,512]{2,1,0:T(4,128)S(1)} %fusion.97, bf16[2,4,2048]{2,1,0:T(4,128)(2,1)S(1)} %convert_element_type.53, bf16[2,512,2048]{2,1,0:T(8,128)(2,1)} %param.8), kind=kOutput, calls=%fused_computation.28 | convolution fusion | flops 33636352 | bytes 8503296 | tf_op jit(solution)/shard_map/esh,edh->esd/dot_general | solution.py:118
  291.3 0.9 broadcast_in_dim.10
  292.2 3.5 all-to-all-start.4
  295.7 2.8 fusion.15
  298.6 5.9 %all-to-all-done.4 = f32[8,2,4,2048]{3,2,1,0:T(4,128)S(1)} async-done(((f32[8,2,4,2048]{3,2,1,0:T(4,128)}), f32[8,2,4,2048]{3,2,1,0:T(4,128)S(1)}, u32[]{:S(2)}, u32[]{:S(2)}) %all-to-all-start.4) | async-done | bytes 524320 | tf_op jit(solution)/shard_map/all_to_all | solution.py:28
  304.4 0.9 broadcast_in_dim.22
  305.3 3.6 all-to-all-start.5
  308.9 0.0 all-gather.15.cloned.1.call-start
  309.0 0.1 reduce_sum.114
  309.1 0.6 convert_element_type.58
  309.7 0.0 all-gather.15.cloned.1.call-update
  309.7 7.8 %all-to-all-done.5 = f32[8,2,4,2048]{3,2,1,0:T(4,128)S(1)} async-done(((f32[8,2,4,2048]{3,2,1,0:T(4,128)}), f32[8,2,4,2048]{3,2,1,0:T(4,128)S(1)}, u32[]{:S(2)}, u32[]{:S(2)}) %all-to-all-start.5) | async-done | bytes 524320 | tf_op jit(solution)/shard_map/all_to_all | solution.py:28
  317.6 0.1 reduce_sum.116
  317.7 1.1 stack.3
  318.8 6.0 %all-to-all-start.6 = ((bf16[32,8,2048]{2,1,0:T(8,128)(2,1)}), bf16[32,8,2048]{2,1,0:T(8,128)(2,1)S(1)}, u32[]{:S(2)}, u32[]{:S(2)}) async-start(bf16[32,8,2048]{2,1,0:T(8,128)(2,1)} %stack.3), calls=%async_computation.6 | async-start | bytes 2097152 | tf_op jit(solution)/shard_map/all_to_all | solution.py:110
  324.8 62.5 %all-gather.15.cloned.1.call-done = bf16[256,2048]{1,0:T(8,128)(2,1)} async-done(((bf16[8,2048]{1,0:T(8,128)(2,1)}), bf16[256,2048]{1,0:T(8,128)(2,1)}) %all-gather.15.cloned.1.call-update) | async-done | bytes 1048592 | tf_op jit(solution)/shard_map/all_gather | solution.py:120
  387.3 2.4 multiply_reduce_fusion.1
  389.7 10.4 %psum.35 = f32[256]{0:T(256)S(1)} all-reduce(f32[256]{0:T(256)S(1)} %get-tuple-element.23), channel_id=1, replica_groups=mesh['seq_0'=4,'seq_1'=2,'exp_0'=8,'exp_1'=2,'exp_2'=2] {'seq_0'}, use_global_device_ids=true, to_apply=%region_10.11 | all-reduce | flops 256 | bytes 2048 | tf_op jit(solution)/shard_map/psum | solution.py:62
  400.1 4.9 psum.36
  405.0 15.6 %psum.37 = f32[256]{0:T(256)S(1)} all-reduce(f32[256]{0:T(256)S(1)} %psum.36), channel_id=1, replica_groups=mesh['seq_0'=4,'seq_1'=2,'exp_0'=8,'exp_1'=2,'exp_2'=2] {'exp_0'}, use_global_device_ids=true, to_apply=%region_12.13 | all-reduce | flops 256 | bytes 2048 | tf_op jit(solution)/shard_map/psum | solution.py:62
  420.6 6.4 %psum.38 = f32[256]{0:T(256)S(1)} all-reduce(f32[256]{0:T(256)S(1)} %psum.37), channel_id=1, replica_groups=mesh['seq_0'=4,'seq_1'=2,'exp_0'=8,'exp_1'=2,'exp_2'=2] {'exp_1'}, use_global_device_ids=true, to_apply=%region_13.14 | all-reduce | flops 256 | bytes 2048 | tf_op jit(solution)/shard_map/psum | solution.py:62
  427.0 2.4 psum.39
  429.5 0.0 all-to-all-done.6
  429.5 0.0 copy-done.2
  429.5 0.6 multiply_reduce_fusion
  430.0 0.7 copy-done.3
  430.7 2.9 convolution_bitcast_fusion
  433.6 8.6 %all-to-all-start.7 = ((f32[32,2048,8]{1,2,0:T(8,128)}), f32[32,2048,8]{1,2,0:T(8,128)S(1)}, u32[]{:S(2)}, u32[]{:S(2)}) async-start(f32[32,2048,8]{1,2,0:T(8,128)} %convolution_bitcast_fusion), calls=%async_computation.7 | async-start | bytes 4194304 | tf_op jit(solution)/shard_map/all_to_all | solution.py:22
  442.2 3.0 fusion.94
  445.2 47.1 %all-to-all-done.7 = f32[32,2048,8]{1,2,0:T(8,128)S(1)} async-done(((f32[32,2048,8]{1,2,0:T(8,128)}), f32[32,2048,8]{1,2,0:T(8,128)S(1)}, u32[]{:S(2)}, u32[]{:S(2)}) %all-to-all-start.7) | async-done | bytes 2097184 | tf_op jit(solution)/shard_map/all_to_all | solution.py:22
  492.4 0.7 reduce_sum.118
  493.1 3.3 all-to-all-start.8
  496.5 3.6 fusion
  500.1 2.7 all-to-all-done.8
  502.7 0.6 reduce_sum.119
  (18 shorter events, 0.2 us)
Async XLA Ops:
  7.2 82.5 %copy-start = (bf16[256,2048]{1,0:T(8,128)(2,1)S(1)}, bf16[256,2048]{1,0:T(8,128)(2,1)}, u32[]{:S(2)}) copy-start(bf16[256,2048]{1,0:T(8,128)(2,1)} %param.5) | copy-start | bytes 3145732
  7.2 82.5 %all-gather.13.cloned.1.call-start = ((), (), s32[]{:S(2)}) async-start(), calls=%async_computation.9 | async-start | bytes 1081344 | tf_op jit(solution)/shard_map/all_gather | solution.py:93
  138.4 57.3 %all-to-all-start.2 = ((f32[32,8,2048]{2,1,0:T(8,128)}), f32[32,8,2048]{2,1,0:T(8,128)S(1)}, u32[]{:S(2)}, u32[]{:S(2)}) async-start(f32[32,8,2048]{2,1,0:T(8,128)} %convolution_bitcast_fusion.1), calls=%async_computation.2 | async-start | bytes 4194304 | tf_op jit(solution)/shard_map/all_to_all | solution.py:22
  195.7 1.3 copy-start.1
  197.0 56.4 %all-to-all-start = ((f32[32,8,2048]{2,1,0:T(8,128)}), f32[32,8,2048]{2,1,0:T(8,128)S(1)}, u32[]{:S(2)}, u32[]{:S(2)}) async-start(f32[32,8,2048]{2,1,0:T(8,128)} %convolution_bitcast_fusion.2), calls=%async_computation | async-start | bytes 4194304 | tf_op jit(solution)/shard_map/all_to_all | solution.py:22
  254.3 14.8 %all-to-all-start.3 = ((f32[8,8,2048]{2,1,0:T(8,128)}), f32[8,8,2048]{2,1,0:T(8,128)}, u32[]{:S(2)}, u32[]{:S(2)}) async-start(f32[8,8,2048]{2,1,0:T(8,128)} %broadcast_in_dim.9), calls=%async_computation.3 | async-start | bytes 1048576 | tf_op jit(solution)/shard_map/all_to_all | solution.py:28
  269.9 12.8 %all-to-all-start.1 = ((f32[8,8,2048]{2,1,0:T(8,128)}), f32[8,8,2048]{2,1,0:T(8,128)S(1)}, u32[]{:S(2)}, u32[]{:S(2)}) async-start(f32[8,8,2048]{2,1,0:T(8,128)} %broadcast_in_dim.8), calls=%async_computation.1 | async-start | bytes 1048576 | tf_op jit(solution)/shard_map/all_to_all | solution.py:28
  292.2 12.2 %all-to-all-start.4 = ((f32[8,2,4,2048]{3,2,1,0:T(4,128)}), f32[8,2,4,2048]{3,2,1,0:T(4,128)S(1)}, u32[]{:S(2)}, u32[]{:S(2)}) async-start(f32[8,2,4,2048]{3,2,1,0:T(4,128)} %broadcast_in_dim.10), calls=%async_computation.4 | async-start | bytes 1048576 | tf_op jit(solution)/shard_map/all_to_all | solution.py:28
  305.3 124.2 %copy-start.2 = (bf16[256,2048]{1,0:T(8,128)(2,1)S(1)}, bf16[256,2048]{1,0:T(8,128)(2,1)}, u32[]{:S(2)}) copy-start(bf16[256,2048]{1,0:T(8,128)(2,1)} %param.9) | copy-start | bytes 3145732
  305.3 12.3 %all-to-all-start.5 = ((f32[8,2,4,2048]{3,2,1,0:T(4,128)}), f32[8,2,4,2048]{3,2,1,0:T(4,128)S(1)}, u32[]{:S(2)}, u32[]{:S(2)}) async-start(f32[8,2,4,2048]{3,2,1,0:T(4,128)} %broadcast_in_dim.22), calls=%async_computation.5 | async-start | bytes 1048576 | tf_op jit(solution)/shard_map/all_to_all | solution.py:28
  308.9 78.3 %all-gather.15.cloned.1.call-start = ((), (), s32[]{:S(2)}) async-start(), calls=%async_computation.10 | async-start | bytes 1081344 | tf_op jit(solution)/shard_map/all_gather | solution.py:120
  318.8 110.7 %all-to-all-start.6 = ((bf16[32,8,2048]{2,1,0:T(8,128)(2,1)}), bf16[32,8,2048]{2,1,0:T(8,128)(2,1)S(1)}, u32[]{:S(2)}, u32[]{:S(2)}) async-start(bf16[32,8,2048]{2,1,0:T(8,128)(2,1)} %stack.3), calls=%async_computation.6 | async-start | bytes 2097152 | tf_op jit(solution)/shard_map/all_to_all | solution.py:110
  430.0 0.7 copy-start.3
  433.6 58.8 %all-to-all-start.7 = ((f32[32,2048,8]{1,2,0:T(8,128)}), f32[32,2048,8]{1,2,0:T(8,128)S(1)}, u32[]{:S(2)}, u32[]{:S(2)}) async-start(f32[32,2048,8]{1,2,0:T(8,128)} %convolution_bitcast_fusion), calls=%async_computation.7 | async-start | bytes 4194304 | tf_op jit(solution)/shard_map/all_to_all | solution.py:22
  493.1 9.6 %all-to-all-start.8 = ((f32[8,256,8]{1,2,0:T(8,128)}), f32[8,256,8]{1,2,0:T(8,128)S(1)}, u32[]{:S(2)}, u32[]{:S(2)}) async-start(f32[8,256,8]{1,2,0:T(8,128)} %bitcast.51), calls=%async_computation.8 | async-start | bytes 131072 | tf_op jit(solution)/shard_map/all_to_all | solution.py:22
Sparse Core Ops, SparseCore 0:
  10.8 78.8 all-gather.12
  312.5 74.6 all-gather.14
